TPU v7x, 32 devices: a whole 2x2x4 slice. The times are simulated.
32 devices in a mesh: seq: 4 (over y, x), sample: 2 (over core), head: 4 (over z).
Axes of the slice: x: 2, y: 2, z: 4, core: 2. Of those that a mesh axis runs over, the one named last changes fastest.
Arguments:
- block_in: bfloat16 [4, 2048, 1024], P('sample', 'seq'), may hold values from -6 to 6
- out_cotangent: bfloat16 [4, 2048, 1024], P('sample', 'seq'), may hold values from -6 to 6
- norm_gain: float32 [1024], replicated, may hold values from 0.25 to 1.75
- gate_proj: bfloat16 [1024, 2048], P(None, 'head'), may hold values from -0.296875 to 0.296875
- value_proj: bfloat16 [1024, 2048], P(None, 'head'), may hold values from -0.1875 to 0.1875
- state_proj: bfloat16 [2, 1024, 128], P(None, None, 'head'), may hold values from -0.1875 to 0.1875
- step_proj: bfloat16 [1024, 32], P(None, 'head'), may hold values from -0.1875 to 0.1875
- conv_value: float32 [4, 2048], P(None, 'head'), may hold values from -0.6 to 0.6
- conv_state: float32 [4, 2, 128], P(None, None, 'head'), may hold values from -0.6 to 0.6
- conv_value_bias: float32 [2048], P('head'), may hold values from -0.5 to 0.5
- conv_state_bias: float32 [2, 128], P(None, 'head'), may hold values from -0.5 to 0.5
- step_bias: float32 [32], P('head'), may hold values from -4.5 to -3
- decay_log: float32 [32], P('head'), may hold values from -10 to 1
- skip_gain: float32 [32], P('head'), may hold values from 0.5 to 1.5
- gated_gain: float32 [2048], P('head'), may hold values from 0.25 to 1.75
- out_proj: bfloat16 [2048, 1024], P('head'), may hold values from -0.125 to 0.125
Outputs:
- block_out: bfloat16 [4, 2048, 1024], P('sample', 'seq')
- input_grad: float32 [4, 2048, 1024], P('sample', 'seq')
- norm_gain_grad: float32 [1024], replicated
- gate_proj_grad: float32 [1024, 2048], P(None, 'head')
- value_proj_grad: float32 [1024, 2048], P(None, 'head')
- state_proj_grad: float32 [2, 1024, 128], P(None, None, 'head')
- step_proj_grad: float32 [1024, 32], P(None, 'head')
- conv_value_grad: float32 [4, 2048], P(None, 'head')
- conv_state_grad: float32 [4, 2, 128], P(None, None, 'head')
- conv_value_bias_grad: float32 [2048], P('head')
- conv_state_bias_grad: float32 [2, 128], P(None, 'head')
- step_bias_grad: float32 [32], P('head')
- decay_log_grad: float32 [32], P('head')
- skip_gain_grad: float32 [32], P('head')
- gated_gain_grad: float32 [2048], P('head')
- out_proj_grad: float32 [2048, 1024], P('head')
All inputs are finite; a program needn't handle non-finite values.
Results may differ from a plain program's by a relative error of at most 0.0055.
The roundings to bfloat16 on the way count: a program that leaves them out, or rounds other values in their place, can miss the bound.
Values may be sent and summed in bfloat16 or wider, within the bound.
A program may use at most 192 MiB of HBM per device.

v0:
```python
import jax
import jax.numpy as jnp
from jax import lax
from jax.sharding import PartitionSpec as P

GROUP = 256
highest = lax.Precision.HIGHEST


def shifted(array, axis, by):
    size = lax.axis_size(axis)
    pairs = [(i, i + by) for i in range(size) if 0 <= i + by < size]
    return lax.ppermute(array, axis, pairs)


def entering(part, axis, combine, identity, reverse):
    count = lax.axis_size(axis)
    place = lax.axis_index(axis)
    ahead = count - 1 - place if reverse else place
    gathered = jax.tree.map(lambda a: lax.all_gather(a, axis), part)
    state = jax.tree.map(lambda a, e: jnp.zeros_like(a) + jnp.asarray(e, a.dtype), part, identity)

    def one(hop, state):
        source = count - 1 - hop if reverse else hop
        return combine(
            state, jax.tree.map(lambda a: lax.dynamic_index_in_dim(a, source, 0, False), gathered)
        )

    return lax.fori_loop(0, ahead, one, state)


def group_pass(values, input_vectors, readout, step_sizes, decay_rates, skip_gain, initial):
    total_length, local_heads, head_width = values.shape
    block_count = total_length // GROUP
    state_width = input_vectors.shape[-1]
    value_blocks = values.reshape(block_count, GROUP, local_heads, head_width)
    input_blocks = input_vectors.reshape(block_count, GROUP, state_width)
    readout_blocks = readout.reshape(block_count, GROUP, state_width)
    step_blocks = step_sizes.reshape(block_count, GROUP, local_heads)
    row_index = lax.broadcasted_iota(jnp.int32, (GROUP, GROUP), 0)
    column_index = lax.broadcasted_iota(jnp.int32, (GROUP, GROUP), 1)
    causal = (row_index >= column_index)[:, :, None]

    def advance(carried_state, block_item):
        block_values, block_inputs, block_readout, block_steps = block_item
        cumulative = jnp.cumsum(block_steps * decay_rates[None, :], axis=0)
        log_gaps = jnp.where(causal, cumulative[:, None, :] - cumulative[None, :, :], 0.0)
        decay_weights = jnp.where(causal, jnp.exp(log_gaps), 0.0)
        scores = jnp.dot(block_readout, block_inputs.T, precision=highest)
        mixing = scores[:, :, None] * decay_weights * block_steps[None, :, :]
        within = jnp.einsum("tsh,shp->thp", mixing, block_values, precision=highest)
        carried = jnp.exp(cumulative)[:, :, None] * jnp.einsum(
            "tn,hpn->thp", block_readout, carried_state, precision=highest
        )
        outputs = within + carried + skip_gain[None, :, None] * block_values
        tail_weight = jnp.exp(cumulative[-1:, :] - cumulative) * block_steps
        next_state = jnp.exp(cumulative[-1])[:, None, None] * carried_state + jnp.einsum(
            "sh,sn,shp->hpn", tail_weight, block_inputs, block_values, precision=highest
        )
        return (next_state, (outputs, cumulative))

    final_state, (outputs, cumulatives) = lax.scan(
        advance, initial, (value_blocks, input_blocks, readout_blocks, step_blocks)
    )
    return (outputs.reshape(total_length, local_heads, head_width), final_state, cumulatives)


def mixer(values, input_vectors, readout, step_raw, step_bias, decay_log, skip_gain, initial):
    step_sizes = jax.nn.softplus(step_raw + step_bias[None, :])
    decay_rates = -jnp.exp(decay_log)
    outputs, final_state, cumulatives = group_pass(
        values, input_vectors, readout, step_sizes, decay_rates, skip_gain, initial
    )
    return (outputs, final_state)


def batched_mixer(
    values, input_vectors, readout, step_raw, step_bias, decay_log, skip_gain, initial
):
    return jax.vmap(mixer, in_axes=(0, 0, 0, 0, None, None, None, 0))(
        values, input_vectors, readout, step_raw, step_bias, decay_log, skip_gain, initial
    )


def silu_slope(inputs):
    sigmoid_values = jax.nn.sigmoid(inputs)
    return sigmoid_values * (1.0 + inputs * (1.0 - sigmoid_values))


def chain(earlier, later):
    return (earlier[0] * later[0], later[0][:, :, None, None] * earlier[1] + later[1])


def per_device(
    block_in,
    out_cotangent,
    norm_gain,
    gate_proj,
    value_proj,
    state_proj,
    step_proj,
    conv_value,
    conv_state,
    conv_value_bias,
    conv_state_bias,
    step_bias,
    decay_log,
    skip_gain,
    gated_gain,
    out_proj,
):
    sequences, block_length, model_width = block_in.shape
    token_rows = sequences * block_length
    local_heads = step_proj.shape[1]
    inner_width = gate_proj.shape[1]
    head_width = inner_width // local_heads
    state_part = state_proj.shape[2]
    conv_taps = conv_value.shape[0]
    channels = inner_width + 2 * state_part
    full_inner = inner_width * lax.axis_size("head")
    flat_in = block_in.reshape(token_rows, model_width).astype(jnp.float32)
    inv_rms = lax.rsqrt(jnp.mean(flat_in * flat_in, axis=1, keepdims=True) + 1e-05)
    normed = (flat_in * inv_rms * norm_gain[None, :]).astype(jnp.bfloat16)
    gate_pre = jnp.dot(normed, gate_proj, preferred_element_type=jnp.float32).astype(jnp.bfloat16)
    value_pre = jnp.dot(normed, value_proj, preferred_element_type=jnp.float32).astype(jnp.bfloat16)
    state_pre = jnp.einsum(
        "td,kdn->tkn", normed, state_proj, preferred_element_type=jnp.float32
    ).astype(jnp.bfloat16)
    step_raw = jnp.dot(normed, step_proj, preferred_element_type=jnp.float32).reshape(
        sequences, block_length, local_heads
    )
    conv_in = jnp.concatenate(
        [value_pre, state_pre.reshape(token_rows, 2 * state_part)], axis=1
    ).reshape(sequences, block_length, channels)
    conv_weight = jnp.concatenate(
        [conv_value, conv_state.reshape(conv_taps, 2 * state_part)], axis=1
    )
    conv_bias = jnp.concatenate([conv_value_bias, conv_state_bias.reshape(2 * state_part)])
    edge_rows = shifted(conv_in[:, block_length - (conv_taps - 1) :], "seq", 1)
    padded = jnp.concatenate([edge_rows, conv_in], axis=1).astype(jnp.float32)
    pre_act = jnp.zeros((sequences, block_length, channels), jnp.float32) + conv_bias[None, None, :]
    for tap_index in range(conv_taps):
        pre_act = (
            pre_act
            + conv_weight[tap_index][None, None, :]
            * padded[:, tap_index : tap_index + block_length]
        )
    activated = jax.nn.silu(pre_act).astype(jnp.bfloat16)
    values = (
        activated[:, :, :inner_width]
        .astype(jnp.float32)
        .reshape(sequences, block_length, local_heads, head_width)
    )
    state_local = activated[:, :, inner_width:].reshape(sequences, block_length, 2, state_part)
    state_full = lax.all_gather(state_local, "head", axis=3, tiled=True)
    input_vectors = state_full[:, :, 0].astype(jnp.float32)
    readout = state_full[:, :, 1].astype(jnp.float32)
    step_sizes = jax.nn.softplus(step_raw + step_bias[None, None, :])
    decay_rates = -jnp.exp(decay_log)
    zero_state = jnp.zeros((sequences, local_heads, head_width, readout.shape[-1]), jnp.float32)
    local_out, local_final, cumulatives = jax.vmap(group_pass, in_axes=(0, 0, 0, 0, None, None, 0))(
        values, input_vectors, readout, step_sizes, decay_rates, skip_gain, zero_state
    )
    block_totals = cumulatives[:, :, -1, :]
    offsets = jnp.cumsum(block_totals, axis=1) - block_totals
    through = (cumulatives + offsets[:, :, None, :]).reshape(sequences, block_length, local_heads)
    block_decay = jnp.exp(through[:, -1, :])
    identity = (jnp.ones_like(block_decay), jnp.zeros_like(local_final))
    unused_decay, incoming = entering((block_decay, local_final), "seq", chain, identity, False)
    carried = jnp.exp(through)[:, :, :, None] * jnp.einsum(
        "stn,shpn->sthp", readout, incoming, precision=highest
    )
    mixed = (local_out + carried).reshape(token_rows, inner_width)
    gate_value = gate_pre.astype(jnp.float32)
    gate_act = jax.nn.silu(gate_value)
    gated = mixed * gate_act
    total_squares = lax.psum(jnp.sum(gated * gated, axis=1), "head")
    gated_rms = lax.rsqrt(total_squares / full_inner + 1e-05)[:, None]
    gated_norm = (gated * gated_rms * gated_gain[None, :]).astype(jnp.bfloat16)
    share_rows = token_rows // lax.axis_size("head")
    branch_share = lax.psum_scatter(
        jnp.dot(gated_norm, out_proj, preferred_element_type=jnp.float32),
        "head",
        scatter_dimension=0,
        tiled=True,
    )
    own_start = lax.axis_index("head") * share_rows
    own_input = lax.dynamic_slice_in_dim(flat_in, own_start, share_rows, 0)
    out_piece = (own_input + branch_share).astype(jnp.bfloat16)
    block_out = lax.all_gather(out_piece, "head", axis=0, tiled=True).reshape(
        sequences, block_length, model_width
    )
    cotangent = out_cotangent.reshape(token_rows, model_width)
    d_norm_out = jnp.einsum("td,cd->tc", cotangent, out_proj, preferred_element_type=jnp.float32)
    out_proj_grad = jnp.einsum(
        "tc,td->cd", gated_norm, cotangent, preferred_element_type=jnp.float32
    )
    gated_gain_grad = jnp.sum(d_norm_out * gated * gated_rms, axis=0)
    scaled = d_norm_out * gated_gain[None, :]
    total_dot = lax.psum(jnp.sum(scaled * gated, axis=1), "head")
    d_gated = gated_rms * scaled - gated * gated_rms**3 * (total_dot / full_inner)[:, None]
    d_mixed = (d_gated * gate_act).reshape(sequences, block_length, local_heads, head_width)
    d_gate = (d_gated * mixed * silu_slope(gate_value)).astype(jnp.bfloat16)
    direct = jnp.einsum("sth,sthp,stn->shpn", jnp.exp(through), d_mixed, readout, precision=highest)
    unused_back, onward = entering((block_decay, direct), "seq", chain, identity, True)
    primal, pullback = jax.vjp(
        batched_mixer,
        values,
        input_vectors,
        readout,
        step_raw,
        step_bias,
        decay_log,
        skip_gain,
        incoming,
    )
    (
        d_values,
        d_inputs,
        d_readout,
        d_step_raw,
        step_bias_grad,
        decay_grad,
        skip_grad,
        unused_state,
    ) = pullback((d_mixed, onward))
    d_state = lax.psum_scatter(
        jnp.stack([d_inputs, d_readout], axis=2), "head", scatter_dimension=3, tiled=True
    )
    d_act = jnp.concatenate(
        [
            d_values.reshape(sequences, block_length, inner_width),
            d_state.reshape(sequences, block_length, 2 * state_part),
        ],
        axis=2,
    )
    d_pre = d_act * silu_slope(pre_act)
    next_rows = shifted(d_pre[:, : conv_taps - 1], "seq", -1)
    d_extended = jnp.concatenate([d_pre, next_rows], axis=1)
    d_conv_in = jnp.zeros_like(d_pre)
    conv_terms = []
    for tap_index in range(conv_taps):
        offset = conv_taps - 1 - tap_index
        d_conv_in = (
            d_conv_in
            + conv_weight[tap_index][None, None, :] * d_extended[:, offset : offset + block_length]
        )
        conv_terms.append(
            jnp.sum(d_pre * padded[:, tap_index : tap_index + block_length], axis=(0, 1))
        )
    conv_grad = jnp.stack(conv_terms)
    conv_bias_grad = jnp.sum(d_pre, axis=(0, 1))
    d_conv_flat = d_conv_in.reshape(token_rows, channels).astype(jnp.bfloat16)
    d_value_pre = d_conv_flat[:, :inner_width]
    d_state_pre = d_conv_flat[:, inner_width:].reshape(token_rows, 2, state_part)
    d_step = d_step_raw.reshape(token_rows, local_heads).astype(jnp.bfloat16)
    gate_grad = jnp.einsum("td,tc->dc", normed, d_gate, preferred_element_type=jnp.float32)
    value_grad = jnp.einsum("td,tc->dc", normed, d_value_pre, preferred_element_type=jnp.float32)
    state_grad = jnp.einsum("td,tkn->kdn", normed, d_state_pre, preferred_element_type=jnp.float32)
    step_grad = jnp.einsum("td,th->dh", normed, d_step, preferred_element_type=jnp.float32)
    partial_normed = jnp.einsum("tc,dc->td", d_gate, gate_proj, preferred_element_type=jnp.float32)
    partial_normed = partial_normed + jnp.einsum(
        "tc,dc->td", d_value_pre, value_proj, preferred_element_type=jnp.float32
    )
    partial_normed = partial_normed + jnp.einsum(
        "tkn,kdn->td", d_state_pre, state_proj, preferred_element_type=jnp.float32
    )
    partial_normed = partial_normed + jnp.einsum(
        "th,dh->td", d_step, step_proj, preferred_element_type=jnp.float32
    )
    d_normed = lax.psum(partial_normed, "head")
    norm_grad = jnp.sum(d_normed * flat_in * inv_rms, axis=0)
    scaled_in = d_normed * norm_gain[None, :]
    input_grad = (
        cotangent.astype(jnp.float32)
        + inv_rms * scaled_in
        - flat_in * inv_rms**3 * jnp.mean(scaled_in * flat_in, axis=1, keepdims=True)
    )
    conv_value_grad = conv_grad[:, :inner_width]
    conv_state_grad = conv_grad[:, inner_width:].reshape(conv_taps, 2, state_part)
    conv_value_bias_grad = conv_bias_grad[:inner_width]
    conv_state_bias_grad = conv_bias_grad[inner_width:].reshape(2, state_part)
    summed = tuple(
        lax.psum(
            (
                norm_grad,
                gate_grad,
                value_grad,
                state_grad,
                step_grad,
                conv_value_grad,
                conv_state_grad,
                conv_value_bias_grad,
                conv_state_bias_grad,
                step_bias_grad,
                decay_grad,
                skip_grad,
                gated_gain_grad,
                out_proj_grad,
            ),
            ("seq", "sample"),
        )
    )
    return (block_out, input_grad.reshape(sequences, block_length, model_width)) + summed


def solution(mesh):
    return jax.shard_map(
        per_device,
        mesh=mesh,
        in_specs=(
            P("sample", "seq", None),
            P("sample", "seq", None),
            P(),
            P(None, "head"),
            P(None, "head"),
            P(None, None, "head"),
            P(None, "head"),
            P(None, "head"),
            P(None, None, "head"),
            P("head"),
            P(None, "head"),
            P("head"),
            P("head"),
            P("head"),
            P("head"),
            P("head", None),
        ),
        out_specs=(
            P("sample", "seq", None),
            P("sample", "seq", None),
            P(),
            P(None, "head"),
            P(None, "head"),
            P(None, None, "head"),
            P(None, "head"),
            P(None, "head"),
            P(None, None, "head"),
            P("head"),
            P(None, "head"),
            P("head"),
            P("head"),
            P("head"),
            P("head"),
            P("head", None),
        ),
        check_vma=False,
    )
```

profile of v0, /device:TPU:0, one launch (start us, length us, event | category | flops | bytes accessed | tf_op | source)
XLA Modules:
  0.0 856.5 jit_solution(13407658360489493288)
XLA Ops:
  36.5 15.6 %all_gather.24 = bf16[2,512,2,128]{1,2,0,3:T(2,128)(2,1)S(1)} all-gather(bf16[2,512,2,32]{1,2,0,3:T(2,128)(2,1)S(1)} %copy.200), channel_id=1, replica_groups=mesh['seq'=4,'sample'=2,'head'=4] {'head'}, dimensions={3}, use_global_device_ids=true | all-gather | bytes 655360 | tf_op jit(solution)/shard_map/all_gather | solution.py:155
  68.6 29.9 %while.120 = (s32[]{:T(128)}, f32[2,8,64,128]{3,2,1,0:T(8,128)}, f32[2,2,256,8,64]{2,4,3,1,0:T(8,128)}, f32[2,2,256,8]{2,3,1,0:T(8,128)S(1)}, f32[2,2,256,8]{2,3...) while((s32[]{:T(128)}, f32[2,8,64,128]{3,2,1,0:T(8,128)}, ...), condition=%wide.region_4.5_spmd.clone.clone, body=%wide.region_1.4_spmd.clone.clone.sunk | while | flops 1819623424 | bytes 16686640 | solution.py:62
  104.1 10.1 %all-gather = f32[8,1,8]{2,1,0:T(1,128)S(1)} all-gather(f32[2,1,8]{2,1,0:T(1,128)S(1)} %slice_exponential_fusion), channel_id=2, replica_groups=mesh['seq'=4,'sample'=2,'head'=4] {'seq'}, dimensions={0}, use_global_device_ids=true | all-gather | bytes 320 | tf_op jit(solution)/shard_map/all_gather | solution.py:20
  121.1 15.5 %all-gather.9.cloned.1.call-done = f32[8,8,64,128]{3,2,1,0:T(8,128)} async-done(((f32[2,8,64,128]{3,2,1,0:T(8,128)}), f32[8,8,64,128]{3,2,1,0:T(8,128)}) %all-gather.9.cloned.1.call-update) | async-done | bytes 2097168 | tf_op jit(solution)/shard_map/all_gather | solution.py:20
  147.2 11.7 %psum.119 = f32[1024]{0:T(1024)S(1)} all-reduce(f32[1024]{0:T(1024)S(1)} %get-tuple-element.2065), channel_id=1, replica_groups=mesh['seq'=4,'sample'=2,'head'=4] {'head'}, use_global_device_ids=true, to_apply=%region_9.10 | all-reduce | flops 1024 | bytes 8192 | tf_op jit(solution)/shard_map/psum | solution.py:177
  158.9 6.2 multiply_reduce_fusion.7
  165.1 8.3 psum.120
  191.7 43.1 %while.119 = (s32[]{:T(128)}, f32[2,8,64,128]{3,2,1,0:T(8,128)}, f32[2,2,256,256,8]{3,4,2,1,0:T(8,128)}, f32[2,2,128,256]{2,3,1,0:T(8,128)}, f32[2,2,256,256,8]{...) while((s32[]{:T(128)}, f32[2,8,64,128]{3,2,1,0:T(8,128)}, ...), condition=%wide.region_18.19_spmd.clone.clone, body=%wide.region_15.18_spmd.clone.clone.sunk | while | flops 1013198912 | bytes 70188120 | solution.py:62
  196.4 6.8 multiply_dynamic-update-slice_fusion.2
  218.1 6.6 multiply_dynamic-update-slice_fusion.2
  243.0 6.3 while.118
  253.5 137.8 %while.121 = (s32[]{:T(128)}, f32[8]{0:T(128)}, f32[8]{0:T(128)}, f32[2,8,64,128]{3,2,1,0:T(8,128)}, f32[2,2,256,8,64]{2,4,3,1,0:T(8,128)}, /*index=5*/f32[2,2,2...) while((s32[]{:T(128)}, f32[8]{0:T(128)}, f32[8]{0:T(128)}, ...), condition=%wide.region_31.32_spmd.clone.clone, body=%wide.region_19.31_spmd.clone.clone.sunk | while | flops 3639656448 | bytes 113358104 | solution.py:62
  253.9 6.0 constant_dynamic-slice_fusion.13
  264.9 10.5 %fusion.281 = (f32[2,256,8]{1,2,0:T(8,128)S(1)}, f32[2,256,8]{1,2,0:T(8,128)S(1)}, f32[2,256,256]{2,1,0:T(8,128)}, f32[2,256,8]{1,2,0:T(8,128)S(1)}) fusion(f32[1,2,256,256,8]{3,4,2,1,0:T(8,128)S(1)} %get-tuple-element.2591, f32[2,256,8]{1,2,0:T(8,128)S(1)} %dynamic-slice_bitcast_fusion.18, f32[2,256,256]{2,1,0:T(8,128)S(1)} %dynamic-slice_bitcast_fusion.19, ...), kind=kOutput, calls=%fused_computation.155.clone.1 | convolution fusion | flops 816697344 | bytes 15860736 | tf_op jit(solution)/shard_map/transpose(jvp(vmap()))/while/body/eval_jaxpr/tsh,shp->thp/dot_general | solution.py:51
  322.6 6.0 constant_dynamic-slice_fusion.13
  333.6 10.5 %fusion.281 = (f32[2,256,8]{1,2,0:T(8,128)S(1)}, f32[2,256,8]{1,2,0:T(8,128)S(1)}, f32[2,256,256]{2,1,0:T(8,128)}, f32[2,256,8]{1,2,0:T(8,128)S(1)}) fusion(f32[1,2,256,256,8]{3,4,2,1,0:T(8,128)S(1)} %get-tuple-element.2591, f32[2,256,8]{1,2,0:T(8,128)S(1)} %dynamic-slice_bitcast_fusion.18, f32[2,256,256]{2,1,0:T(8,128)S(1)} %dynamic-slice_bitcast_fusion.19, ...), kind=kOutput, calls=%fused_computation.155.clone.1 | convolution fusion | flops 816697344 | bytes 15860736 | tf_op jit(solution)/shard_map/transpose(jvp(vmap()))/while/body/eval_jaxpr/tsh,shp->thp/dot_general | solution.py:51
  415.0 31.8 %all-reduce.11.cloned.1.call-done = f32[2,512,2,128]{1,2,0,3:T(2,128)} async-done(((f32[2,512,2,128]{1,2,0,3:T(2,128)}), f32[2,512,2,128]{1,2,0,3:T(2,128)}) %all-reduce.11.cloned.1.call-update) | async-done | bytes 1048592
  447.9 8.2 multiply_reduce_fusion.6
  463.7 6.2 fusion.151
  481.2 44.4 %reduce-scatter.2.cloned.1.call-done = f32[256,1024]{1,0:T(8,128)} async-done(((f32[1024,1024]{1,0:T(8,128)}), f32[256,1024]{1,0:T(8,128)}) %reduce-scatter.2.cloned.1.call-update) | async-done | bytes 1048592 | tf_op jit(solution)/shard_map/reduce_scatter | solution.py:181
  543.0 140.4 %all-reduce.9.cloned.1.call-done = f32[1024,1024]{1,0:T(8,128)} async-done(((f32[1024,1024]{1,0:T(8,128)}), f32[1024,1024]{1,0:T(8,128)}) %all-reduce.9.cloned.1.call-update) | async-done | bytes 4194320 | tf_op jit(solution)/shard_map/psum | solution.py:271
  686.9 26.1 %all-reduce.3 = (f32[1024]{0:T(1024)}, f32[1024,8]{0,1:T(8,128)}, f32[4,512]{1,0:T(4,128)}, f32[4,2,32]{2,1,0:T(2,128)}, f32[512]{0:T(512)}, /*index=5*/f32[2,32...) all-reduce(f32[1024]{0:T(1024)S(1)} %get-tuple-element.1844, ...), channel_id=1, replica_groups=mesh['seq'=4,'sample'=2,'head'=4] {'seq','sample'}, use_global_device_ids=true, to_apply=%region_36.37 | all-reduce | flops 12632 | bytes 101056 | tf_op jit(solution)/shard_map/psum | solution.py:284
  717.8 11.6 %all-gather.7.cloned.1.call-done = bf16[1024,1024]{1,0:T(8,128)(2,1)} async-done(((bf16[256,1024]{1,0:T(8,128)(2,1)}), bf16[1024,1024]{1,0:T(8,128)(2,1)}) %all-gather.7.cloned.1.call-update) | async-done | bytes 2097168 | tf_op jit(solution)/shard_map/all_gather | solution.py:190
  729.4 110.5 %all-reduce.13.cloned.1.call-done = (f32[1024,512]{1,0:T(8,128)}, f32[1024,512]{1,0:T(8,128)}, f32[2,1024,32]{1,2,0:T(8,128)}, f32[512,1024]{1,0:T(8,128)}) async-done(((f32[1024,512]{1,0:T(8,128)}, f32[1024,512]{1,0:T(8,128)}, f32[2,1024,32]{1,2,0:T(8,128)}, f32[512,1024]{1,0:T(8,128)}), (f32[1024,512]{1,0:T(8,128)}, f32[1024,512]{1,0:T(8,128)}, f32[2,1024,32]{1,2,0:T(8,128)}, ...) | async-done | bytes 6553616 | tf_op jit(solution)/shard_map/psum | solution.py:284
  (590 shorter events, 345.9 us)
Async XLA Ops:
  7.2 151.7 %copy-start = (bf16[512,1024]{1,0:T(8,128)(2,1)S(1)}, bf16[512,1024]{1,0:T(8,128)(2,1)}, u32[]{:S(2)}) copy-start(bf16[512,1024]{1,0:T(8,128)(2,1)} %param.41) | copy-start | bytes 3145732
  7.2 129.4 %all-gather.9.cloned.1.call-start = ((), (), s32[]{:S(2)}) async-start(), calls=%async_computation.4 | async-start | bytes 2621440 | tf_op jit(solution)/shard_map/all_gather | solution.py:20
  15.3 9.9 %copy-start.90 = (f32[4,512]{1,0:T(4,128)S(1)}, f32[4,512]{1,0:T(4,128)}, u32[]{:S(2)}) copy-start(f32[4,512]{1,0:T(4,128)} %param.33) | copy-start | bytes 24580
  15.3 9.9 %copy-start.91 = (f32[4,2,32]{2,1,0:T(2,128)S(1)}, f32[4,2,32]{2,1,0:T(2,128)}, u32[]{:S(2)}) copy-start(f32[4,2,32]{2,1,0:T(2,128)} %param.34) | copy-start | bytes 3076
  15.3 10.1 %copy-start.100 = (f32[2,32]{1,0:T(2,128)S(1)}, f32[2,32]{1,0:T(2,128)}, u32[]{:S(2)}) copy-start(f32[2,32]{1,0:T(2,128)} %param.36) | copy-start | bytes 772
  19.7 11.4 %collective-permute-start = (bf16[2,3,576]{1,2,0:T(8,128)(2,1)}, bf16[2,3,576]{1,2,0:T(8,128)(2,1)}, u32[]{:S(2)}, u32[]{:S(2)}) collective-permute-start(bf16[2,3,576]{1,2,0:T(8,128)(2,1)} %pad_maximum_fusion.2), channel_id=1, source_target_pairs={{0,8},{8,16},{16,24},{1,9},{9,17},{17,25},{2,10},{10,18},{18,26},{... | collective-permute-start | bytes 20744 | tf_op jit(solution)/shard_map/ppermute | solution.py:13
  98.5 143.7 %all-gather.11.cloned.1.call-start = ((), (), s32[]{:S(2)}) async-start(), calls=%async_computation.5 | async-start | bytes 2621440 | tf_op jit(solution)/shard_map/all_gather | solution.py:20
  144.6 14.3 %copy-start.92 = (f32[512]{0:T(512)S(1)}, f32[512]{0:T(512)}, u32[]{:S(2)}) copy-start(f32[512]{0:T(512)} %param.40) | copy-start | bytes 6148
  158.9 14.5 %copy-start.79 = (f32[1024]{0:T(1024)}, f32[1024]{0:T(1024)S(1)}, u32[]{:S(2)}) copy-start(f32[1024]{0:T(1024)S(1)} %get-tuple-element.2058) | copy-start | bytes 12292
  186.7 260.1 %all-reduce.11.cloned.1.call-start = ((), (), s32[]{:S(2)}) async-start(), calls=%async_computation.6 | async-start | bytes 2097152
  287.5 15.4 %copy-start.87 = (f32[8]{0:T(128)S(1)}, f32[8]{0:T(128)}, u32[]{:S(2)}) copy-start(f32[8]{0:T(128)} %get-tuple-element.2809) | copy-start | bytes 100 | tf_op jit(solution)/shard_map/transpose(jvp(vmap()))/while
  302.9 9.5 %copy-start.88 = (f32[8]{0:T(128)}, f32[8]{0:T(128)S(1)}, u32[]{:S(2)}) copy-start(f32[8]{0:T(128)S(1)} %fusion.287) | copy-start | bytes 100 | tf_op jit(solution)/shard_map/transpose(jvp(vmap()))/while
  303.7 10.5 %copy-start.9 = (f32[2,256,8,64]{1,3,2,0:T(8,128)S(1)}, f32[2,256,8,64]{1,3,2,0:T(8,128)}, u32[]{:S(2)}) copy-start(f32[2,256,8,64]{1,3,2,0:T(8,128)} %get-tuple-element.2602) | copy-start | bytes 3145732 | tf_op jit(solution)/shard_map/transpose(jvp(vmap()))/while
  356.2 15.4 %copy-start.87 = (f32[8]{0:T(128)S(1)}, f32[8]{0:T(128)}, u32[]{:S(2)}) copy-start(f32[8]{0:T(128)} %get-tuple-element.2809) | copy-start | bytes 100 | tf_op jit(solution)/shard_map/transpose(jvp(vmap()))/while
  371.6 9.5 %copy-start.88 = (f32[8]{0:T(128)}, f32[8]{0:T(128)S(1)}, u32[]{:S(2)}) copy-start(f32[8]{0:T(128)S(1)} %fusion.287) | copy-start | bytes 100 | tf_op jit(solution)/shard_map/transpose(jvp(vmap()))/while
  372.4 10.5 %copy-start.9 = (f32[2,256,8,64]{1,3,2,0:T(8,128)S(1)}, f32[2,256,8,64]{1,3,2,0:T(8,128)}, u32[]{:S(2)}) copy-start(f32[2,256,8,64]{1,3,2,0:T(8,128)} %get-tuple-element.2602) | copy-start | bytes 3145732 | tf_op jit(solution)/shard_map/transpose(jvp(vmap()))/while
  396.1 129.5 %reduce-scatter.2.cloned.1.call-start = ((), (), s32[]{:S(2)}) async-start(), calls=%async_computation.1 | async-start | bytes 5242880 | tf_op jit(solution)/shard_map/reduce_scatter | solution.py:181
  401.0 282.3 %all-reduce.9.cloned.1.call-start = ((), (), s32[]{:S(2)}) async-start(), calls=%async_computation.3 | async-start | bytes 8388608 | tf_op jit(solution)/shard_map/psum | solution.py:271
  457.8 5.6 collective-permute-start.1
  477.0 252.4 %all-gather.7.cloned.1.call-start = ((), (), s32[]{:S(2)}) async-start(), calls=%async_computation.2 | async-start | bytes 2621440 | tf_op jit(solution)/shard_map/all_gather | solution.py:190
  528.1 311.9 %all-reduce.13.cloned.1.call-start = ((), (), s32[]{:S(2)}) async-start(), calls=%async_computation.7 | async-start | bytes 13107200 | tf_op jit(solution)/shard_map/psum | solution.py:284
  540.7 142.7 %copy-start.64 = (f32[1024]{0:T(1024)S(1)}, f32[1024]{0:T(1024)}, u32[]{:S(2)}) copy-start(f32[1024]{0:T(1024)} %param.28) | copy-start | bytes 12292
  543.0 143.9 %copy-start.78 = (f32[8]{0:T(128)S(1)}, f32[8]{0:T(128)}, u32[]{:S(2)}) copy-start(f32[8]{0:T(128)} %get-tuple-element.1204) | copy-start | bytes 100
  543.0 143.9 %copy-start.94 = (f32[512]{0:T(512)S(1)}, f32[512]{0:T(512)}, u32[]{:S(2)}) copy-start(f32[512]{0:T(512)} %get-tuple-element.1850) | copy-start | bytes 6148
  (130 other events, 526.5 us)
Sparse Core Ops, SparseCore 0:
  98.6 37.9 all-gather.8
  186.8 40.2 all-gather.10
  396.2 50.5 all-reduce.10
  449.5 76.0 reduce-scatter.1
  527.8 155.5 all-reduce.8
  684.8 44.6 all-gather.6
  734.2 105.6 all-reduce.12
where the time goes:
time: 865 us; the launch traced here: 856 us
  waiting for transfers between devices  360 us (42%)
  matrix products  155 us (18%)
  local copies, waits for them, and re-layouts  138 us (16%)
  other arithmetic  107 us (12%)
  blocking collectives  71.8 us (8%)
  between operations  15.9 us (2%)
    psum x1, waiting for transfers between devices, per_device(): d_normed = lax.psum(partial_normed, 'head')  140 us
    psum x1, waiting for transfers between devices, per_device(): lax.psum((norm_grad, gate_grad, value_grad, state_grad, step_grad, conv_v...  111 us
    reduce_scatter x1, waiting for transfers between devices, per_device(): lax.psum_scatter(jnp.dot(gated_norm, out_proj, preferred_element_type=jnp...  44.4 us
    dot_general x6, matrix products, advance(): within = jnp.einsum('tsh,shp->thp', mixing, block_values, precision=highest)  42.7 us
    unnamed x8, waiting for transfers between devices  31.9 us
    unnamed x139, local copies, waits for them, and re-layouts  27.6 us
    psum x1, blocking collectives, per_device(): lax.psum((norm_grad, gate_grad, value_grad, state_grad, step_grad, conv_v...  26.1 us
    dynamic_slice x10, local copies, waits for them, and re-layouts, group_pass(): lax.scan(advance, initial, (value_blocks, input_blocks, readout_blocks, s...  25.2 us
  transfers between devices with their start and end apart: 9, of which 8 were waited for; matrix products, arithmetic and copies ran while one was open for 15% of the time, Pallas kernels for 0%

commit v1 on v0

--- a/solution.py
+++ b/solution.py
@@ -5,6 +5,11 @@
 
 GROUP = 256
 highest = lax.Precision.HIGHEST
+
+
+def by_each_axis(array_2, first, second):
+    partial = lax.psum(array_2, first)
+    return lax.psum(partial, second)
 
 
 def shifted(array, axis, by):
@@ -281,7 +286,7 @@
     conv_value_bias_grad = conv_bias_grad[:inner_width]
     conv_state_bias_grad = conv_bias_grad[inner_width:].reshape(2, state_part)
     summed = tuple(
-        lax.psum(
+        by_each_axis(
             (
                 norm_grad,
                 gate_grad,
@@ -298,7 +303,8 @@
                 gated_gain_grad,
                 out_proj_grad,
             ),
-            ("seq", "sample"),
+            "sample",
+            "seq",
         )
     )
     return (block_out, input_grad.reshape(sequences, block_length, model_width)) + summed

time: 865 us -> 938 us (1.084)
  waiting for transfers between devices: 360 us -> 439 us
    psum x1 -> x2, waiting for transfers between devices: 111 us -> 180 us  [the longest x1 145 us: by_each_axis(): return lax.psum(partial, second)]
    psum x1, waiting for transfers between devices: 140 us -> 155 us  [per_device(): d_normed = lax.psum(partial_normed, 'head')]
    reduce_scatter x1, waiting for transfers between devices: 44.4 us -> 33.7 us  [per_device(): lax.psum_scatter(jnp.dot(gated_norm, out_proj, preferred_element_type=jnp...]
    psum x1 -> x2, blocking collectives: 26.1 us -> 21 us  [the longest x1 17.5 us: by_each_axis(): return lax.psum(partial, second)]
    unnamed x8 -> x9, waiting for transfers between devices: 31.9 us -> 34.8 us
    unnamed x139 -> x129, local copies, waits for them, and re-layouts: 27.6 us -> 27.2 us
  transfers between devices with their start and end apart: 9 -> 10, of which waited for: 8 -> 8; matrix products, arithmetic and copies ran while one was open for 15% -> 14% of each run, Pallas kernels for 0% -> 0%
where the time goes in v1:
time: 938 us; the launch traced here: 930 us
  waiting for transfers between devices  439 us (47%)
  matrix products  157 us (17%)
  local copies, waits for them, and re-layouts  137 us (15%)
  other arithmetic  106 us (11%)
  blocking collectives  66.8 us (7%)
  between operations  15.9 us (2%)
    psum x1, waiting for transfers between devices, per_device(): d_normed = lax.psum(partial_normed, 'head')  155 us
    psum x1, waiting for transfers between devices, by_each_axis(): return lax.psum(partial, second)  145 us
    dot_general x6, matrix products, advance(): within = jnp.einsum('tsh,shp->thp', mixing, block_values, precision=highest)  42.8 us
    unnamed x9, waiting for transfers between devices  34.8 us
    psum x1, waiting for transfers between devices, by_each_axis(): partial = lax.psum(array_2, first)  34.7 us
    reduce_scatter x1, waiting for transfers between devices, per_device(): lax.psum_scatter(jnp.dot(gated_norm, out_proj, preferred_element_type=jnp...  33.7 us
    unnamed x129, local copies, waits for them, and re-layouts  27.2 us
    dynamic_slice x10, local copies, waits for them, and re-layouts, group_pass(): lax.scan(advance, initial, (value_blocks, input_blocks, readout_blocks, s...  25.2 us
  transfers between devices with their start and end apart: 10, of which 8 were waited for; matrix products, arithmetic and copies ran while one was open for 14% of the time, Pallas kernels for 0%

profile of v1, /device:TPU:0, one launch (start us, length us, event | category | flops | bytes accessed | tf_op | source)
XLA Modules:
  0.0 930.2 jit_solution(11560503058521303009)
XLA Ops:
  36.5 15.6 %all_gather.24 = bf16[2,512,2,128]{1,2,0,3:T(2,128)(2,1)S(1)} all-gather(bf16[2,512,2,32]{1,2,0,3:T(2,128)(2,1)S(1)} %copy.200), channel_id=1, replica_groups=mesh['seq'=4,'sample'=2,'head'=4] {'head'}, dimensions={3}, use_global_device_ids=true | all-gather | bytes 655360 | tf_op jit(solution)/shard_map/all_gather | solution.py:160
  68.6 29.9 %while.120 = (s32[]{:T(128)}, f32[2,8,64,128]{3,2,1,0:T(8,128)}, f32[2,2,256,8,64]{2,4,3,1,0:T(8,128)}, f32[2,2,256,8]{2,3,1,0:T(8,128)S(1)}, f32[2,2,256,8]{2,3...) while((s32[]{:T(128)}, f32[2,8,64,128]{3,2,1,0:T(8,128)}, ...), condition=%wide.region_4.5_spmd.clone.clone, body=%wide.region_1.4_spmd.clone.clone.sunk | while | flops 1819623424 | bytes 16686640 | solution.py:67
  104.0 10.1 %all-gather = f32[8,1,8]{2,1,0:T(1,128)S(1)} all-gather(f32[2,1,8]{2,1,0:T(1,128)S(1)} %slice_exponential_fusion), channel_id=2, replica_groups=mesh['seq'=4,'sample'=2,'head'=4] {'seq'}, dimensions={0}, use_global_device_ids=true | all-gather | bytes 320 | tf_op jit(solution)/shard_map/all_gather | solution.py:25
  121.1 15.5 %all-gather.9.cloned.1.call-done = f32[8,8,64,128]{3,2,1,0:T(8,128)} async-done(((f32[2,8,64,128]{3,2,1,0:T(8,128)}), f32[8,8,64,128]{3,2,1,0:T(8,128)}) %all-gather.9.cloned.1.call-update) | async-done | bytes 2097168 | tf_op jit(solution)/shard_map/all_gather | solution.py:25
  147.2 11.7 %psum.217 = f32[1024]{0:T(1024)S(1)} all-reduce(f32[1024]{0:T(1024)S(1)} %get-tuple-element.2079), channel_id=1, replica_groups=mesh['seq'=4,'sample'=2,'head'=4] {'head'}, use_global_device_ids=true, to_apply=%region_9.10 | all-reduce | flops 1024 | bytes 8192 | tf_op jit(solution)/shard_map/psum | solution.py:182
  158.9 6.2 multiply_reduce_fusion.7
  165.1 8.3 psum.218
  191.8 43.2 %while.119 = (s32[]{:T(128)}, f32[2,8,64,128]{3,2,1,0:T(8,128)}, f32[2,2,256,256,8]{3,4,2,1,0:T(8,128)}, f32[2,2,128,256]{2,3,1,0:T(8,128)}, f32[2,2,256,256,8]{...) while((s32[]{:T(128)}, f32[2,8,64,128]{3,2,1,0:T(8,128)}, ...), condition=%wide.region_18.19_spmd.clone.clone, body=%wide.region_15.18_spmd.clone.clone.sunk | while | flops 1013198912 | bytes 70188120 | solution.py:67
  196.5 6.8 multiply_dynamic-update-slice_fusion.2
  218.2 6.6 multiply_dynamic-update-slice_fusion.2
  243.2 6.3 while.118
  253.7 138.0 %while.121 = (s32[]{:T(128)}, f32[8]{0:T(128)}, f32[8]{0:T(128)}, f32[2,8,64,128]{3,2,1,0:T(8,128)}, f32[2,2,256,8,64]{2,4,3,1,0:T(8,128)}, /*index=5*/f32[2,2,2...) while((s32[]{:T(128)}, f32[8]{0:T(128)}, f32[8]{0:T(128)}, ...), condition=%wide.region_31.32_spmd.clone.clone, body=%wide.region_19.31_spmd.clone.clone.sunk | while | flops 3639656448 | bytes 113358104 | solution.py:67
  254.2 6.0 constant_dynamic-slice_fusion.13
  265.2 10.5 %fusion.281 = (f32[2,256,8]{1,2,0:T(8,128)S(1)}, f32[2,256,8]{1,2,0:T(8,128)S(1)}, f32[2,256,256]{2,1,0:T(8,128)}, f32[2,256,8]{1,2,0:T(8,128)S(1)}) fusion(f32[1,2,256,256,8]{3,4,2,1,0:T(8,128)S(1)} %get-tuple-element.2605, f32[2,256,8]{1,2,0:T(8,128)S(1)} %dynamic-slice_bitcast_fusion.18, f32[2,256,256]{2,1,0:T(8,128)S(1)} %dynamic-slice_bitcast_fusion.19, ...), kind=kOutput, calls=%fused_computation.155.clone.1 | convolution fusion | flops 816697344 | bytes 15860736 | tf_op jit(solution)/shard_map/transpose(jvp(vmap()))/while/body/eval_jaxpr/tsh,shp->thp/dot_general | solution.py:56
  322.9 6.0 constant_dynamic-slice_fusion.13
  333.9 10.5 %fusion.281 = (f32[2,256,8]{1,2,0:T(8,128)S(1)}, f32[2,256,8]{1,2,0:T(8,128)S(1)}, f32[2,256,256]{2,1,0:T(8,128)}, f32[2,256,8]{1,2,0:T(8,128)S(1)}) fusion(f32[1,2,256,256,8]{3,4,2,1,0:T(8,128)S(1)} %get-tuple-element.2605, f32[2,256,8]{1,2,0:T(8,128)S(1)} %dynamic-slice_bitcast_fusion.18, f32[2,256,256]{2,1,0:T(8,128)S(1)} %dynamic-slice_bitcast_fusion.19, ...), kind=kOutput, calls=%fused_computation.155.clone.1 | convolution fusion | flops 816697344 | bytes 15860736 | tf_op jit(solution)/shard_map/transpose(jvp(vmap()))/while/body/eval_jaxpr/tsh,shp->thp/dot_general | solution.py:56
  412.5 34.7 %all-reduce.14.cloned.1.call-done = f32[2,512,2,128]{1,2,0,3:T(2,128)} async-done(((f32[2,512,2,128]{1,2,0,3:T(2,128)}), f32[2,512,2,128]{1,2,0,3:T(2,128)}) %all-reduce.14.cloned.1.call-update) | async-done | bytes 1048592
  448.3 8.3 multiply_reduce_fusion.6
  492.4 33.7 %reduce-scatter.2.cloned.1.call-done = f32[256,1024]{1,0:T(8,128)} async-done(((f32[1024,1024]{1,0:T(8,128)}), f32[256,1024]{1,0:T(8,128)}) %reduce-scatter.2.cloned.1.call-update) | async-done | bytes 1048592 | tf_op jit(solution)/shard_map/reduce_scatter | solution.py:186
  528.6 34.7 %all-reduce.18.cloned.1.call-done = (f32[1024,512]{1,0:T(8,128)}, f32[1024,512]{1,0:T(8,128)}, f32[2,1024,32]{1,2,0:T(8,128)}, f32[512,1024]{1,0:T(8,128)}) async-done(((f32[1024,512]{1,0:T(8,128)}, f32[1024,512]{1,0:T(8,128)}, f32[2,1024,32]{1,2,0:T(8,128)}, f32[512,1024]{1,0:T(8,128)}), (f32[1024,512]{1,0:T(8,128)}, f32[1024,512]{1,0:T(8,128)}, f32[2,1024,32]{1,2,0:T(8,128)}, ...) | async-done | bytes 6553616 | tf_op jit(solution)/shard_map/psum | solution.py:11
  566.3 155.4 %all-reduce.12.cloned.1.call-done = f32[1024,1024]{1,0:T(8,128)} async-done(((f32[1024,1024]{1,0:T(8,128)}), f32[1024,1024]{1,0:T(8,128)}) %all-reduce.12.cloned.1.call-update) | async-done | bytes 4194320 | tf_op jit(solution)/shard_map/psum | solution.py:276
  728.9 17.5 %all-reduce.3 = (f32[1024]{0:T(1024)}, f32[1024,8]{0,1:T(8,128)}, f32[4,512]{1,0:T(4,128)}, f32[4,2,32]{2,1,0:T(2,128)}, f32[512]{0:T(512)}, /*index=5*/f32[2,32...) all-reduce(f32[1024]{0:T(1024)S(1)} %get-tuple-element.2023, ...), channel_id=1, replica_groups=mesh['seq'=4,'sample'=2,'head'=4] {'seq'}, use_global_device_ids=true, to_apply=%region_37.38 | all-reduce | flops 12632 | bytes 101056 | tf_op jit(solution)/shard_map/psum | solution.py:12
  751.1 17.4 %all-gather.7.cloned.1.call-done = bf16[1024,1024]{1,0:T(8,128)(2,1)} async-done(((bf16[256,1024]{1,0:T(8,128)(2,1)}), bf16[1024,1024]{1,0:T(8,128)(2,1)}) %all-gather.7.cloned.1.call-update) | async-done | bytes 2097168 | tf_op jit(solution)/shard_map/all_gather | solution.py:195
  768.5 145.2 %all-reduce.16.cloned.1.call-done = (f32[1024,512]{1,0:T(8,128)}, f32[1024,512]{1,0:T(8,128)}, f32[2,1024,32]{1,2,0:T(8,128)}, f32[512,1024]{1,0:T(8,128)}) async-done(((f32[1024,512]{1,0:T(8,128)}, f32[1024,512]{1,0:T(8,128)}, f32[2,1024,32]{1,2,0:T(8,128)}, f32[512,1024]{1,0:T(8,128)}), (f32[1024,512]{1,0:T(8,128)}, f32[1024,512]{1,0:T(8,128)}, f32[2,1024,32]{1,2,0:T(8,128)}, ...) | async-done | bytes 6553616 | tf_op jit(solution)/shard_map/psum | solution.py:12
  (584 shorter events, 352.0 us)
Async XLA Ops:
  7.2 151.7 %copy-start = (bf16[512,1024]{1,0:T(8,128)(2,1)S(1)}, bf16[512,1024]{1,0:T(8,128)(2,1)}, u32[]{:S(2)}) copy-start(bf16[512,1024]{1,0:T(8,128)(2,1)} %param.41) | copy-start | bytes 3145732
  7.2 129.4 %all-gather.9.cloned.1.call-start = ((), (), s32[]{:S(2)}) async-start(), calls=%async_computation.4 | async-start | bytes 2621440 | tf_op jit(solution)/shard_map/all_gather | solution.py:25
  15.3 9.9 %copy-start.85 = (f32[4,512]{1,0:T(4,128)S(1)}, f32[4,512]{1,0:T(4,128)}, u32[]{:S(2)}) copy-start(f32[4,512]{1,0:T(4,128)} %param.33) | copy-start | bytes 24580
  15.3 10.0 %copy-start.86 = (f32[4,2,32]{2,1,0:T(2,128)S(1)}, f32[4,2,32]{2,1,0:T(2,128)}, u32[]{:S(2)}) copy-start(f32[4,2,32]{2,1,0:T(2,128)} %param.34) | copy-start | bytes 3076
  15.3 10.1 %copy-start.95 = (f32[2,32]{1,0:T(2,128)S(1)}, f32[2,32]{1,0:T(2,128)}, u32[]{:S(2)}) copy-start(f32[2,32]{1,0:T(2,128)} %param.36) | copy-start | bytes 772
  19.7 11.4 %collective-permute-start = (bf16[2,3,576]{1,2,0:T(8,128)(2,1)}, bf16[2,3,576]{1,2,0:T(8,128)(2,1)}, u32[]{:S(2)}, u32[]{:S(2)}) collective-permute-start(bf16[2,3,576]{1,2,0:T(8,128)(2,1)} %pad_maximum_fusion.2), channel_id=1, source_target_pairs={{0,8},{8,16},{16,24},{1,9},{9,17},{17,25},{2,10},{10,18},{18,26},{... | collective-permute-start | bytes 20744 | tf_op jit(solution)/shard_map/ppermute | solution.py:18
  98.5 143.9 %all-gather.11.cloned.1.call-start = ((), (), s32[]{:S(2)}) async-start(), calls=%async_computation.5 | async-start | bytes 2621440 | tf_op jit(solution)/shard_map/all_gather | solution.py:25
  144.6 14.3 %copy-start.87 = (f32[512]{0:T(512)S(1)}, f32[512]{0:T(512)}, u32[]{:S(2)}) copy-start(f32[512]{0:T(512)} %param.40) | copy-start | bytes 6148
  158.9 14.5 %copy-start.74 = (f32[1024]{0:T(1024)}, f32[1024]{0:T(1024)S(1)}, u32[]{:S(2)}) copy-start(f32[1024]{0:T(1024)S(1)} %get-tuple-element.2072) | copy-start | bytes 12292
  186.7 260.5 %all-reduce.14.cloned.1.call-start = ((), (), s32[]{:S(2)}) async-start(), calls=%async_computation.6 | async-start | bytes 2097152
  287.8 15.4 %copy-start.82 = (f32[8]{0:T(128)S(1)}, f32[8]{0:T(128)}, u32[]{:S(2)}) copy-start(f32[8]{0:T(128)} %get-tuple-element.2823) | copy-start | bytes 100 | tf_op jit(solution)/shard_map/transpose(jvp(vmap()))/while
  304.0 10.5 %copy-start.9 = (f32[2,256,8,64]{1,3,2,0:T(8,128)S(1)}, f32[2,256,8,64]{1,3,2,0:T(8,128)}, u32[]{:S(2)}) copy-start(f32[2,256,8,64]{1,3,2,0:T(8,128)} %get-tuple-element.2616) | copy-start | bytes 3145732 | tf_op jit(solution)/shard_map/transpose(jvp(vmap()))/while
  356.5 15.3 %copy-start.82 = (f32[8]{0:T(128)S(1)}, f32[8]{0:T(128)}, u32[]{:S(2)}) copy-start(f32[8]{0:T(128)} %get-tuple-element.2823) | copy-start | bytes 100 | tf_op jit(solution)/shard_map/transpose(jvp(vmap()))/while
  371.9 9.5 %copy-start.83 = (f32[8]{0:T(128)}, f32[8]{0:T(128)S(1)}, u32[]{:S(2)}) copy-start(f32[8]{0:T(128)S(1)} %fusion.287) | copy-start | bytes 100 | tf_op jit(solution)/shard_map/transpose(jvp(vmap()))/while
  372.7 10.5 %copy-start.9 = (f32[2,256,8,64]{1,3,2,0:T(8,128)S(1)}, f32[2,256,8,64]{1,3,2,0:T(8,128)}, u32[]{:S(2)}) copy-start(f32[2,256,8,64]{1,3,2,0:T(8,128)} %get-tuple-element.2616) | copy-start | bytes 3145732 | tf_op jit(solution)/shard_map/transpose(jvp(vmap()))/while
  396.5 129.5 %reduce-scatter.2.cloned.1.call-start = ((), (), s32[]{:S(2)}) async-start(), calls=%async_computation.1 | async-start | bytes 5242880 | tf_op jit(solution)/shard_map/reduce_scatter | solution.py:186
  401.5 161.9 %all-reduce.18.cloned.1.call-start = ((), (), s32[]{:S(2)}) async-start(), calls=%async_computation.8 | async-start | bytes 13107200 | tf_op jit(solution)/shard_map/psum | solution.py:11
  458.8 5.8 collective-permute-start.1
  476.0 245.7 %all-reduce.12.cloned.1.call-start = ((), (), s32[]{:S(2)}) async-start(), calls=%async_computation.3 | async-start | bytes 8388608 | tf_op jit(solution)/shard_map/psum | solution.py:276
  488.3 280.3 %all-gather.7.cloned.1.call-start = ((), (), s32[]{:S(2)}) async-start(), calls=%async_computation.2 | async-start | bytes 2621440 | tf_op jit(solution)/shard_map/all_gather | solution.py:195
  528.5 385.2 %all-reduce.16.cloned.1.call-start = ((), (), s32[]{:S(2)}) async-start(), calls=%async_computation.7 | async-start | bytes 13107200 | tf_op jit(solution)/shard_map/psum | solution.py:12
  564.0 157.7 %copy-start.59 = (f32[1024]{0:T(1024)S(1)}, f32[1024]{0:T(1024)}, u32[]{:S(2)}) copy-start(f32[1024]{0:T(1024)} %param.28) | copy-start | bytes 12292
  566.3 159.0 %copy-start.73 = (f32[8]{0:T(128)S(1)}, f32[8]{0:T(128)}, u32[]{:S(2)}) copy-start(f32[8]{0:T(128)} %get-tuple-element.1204) | copy-start | bytes 100
  566.3 159.0 %copy-start.89 = (f32[512]{0:T(512)S(1)}, f32[512]{0:T(512)}, u32[]{:S(2)}) copy-start(f32[512]{0:T(512)} %get-tuple-element.1850) | copy-start | bytes 6148
  (126 other events, 515.5 us)
Sparse Core Ops, SparseCore 0:
  98.6 37.9 all-gather.8
  186.8 40.1 all-gather.10
  396.6 50.5 all-reduce.13
  449.9 76.0 reduce-scatter.1
  529.8 33.4 all-reduce.17
  565.5 156.1 all-reduce.11
  723.9 44.6 all-gather.6
  772.4 141.3 all-reduce.15
